TPU v7x, 128 devices: a whole 4x4x4 slice. The times are simulated.
128 devices in a mesh: row: 8 (over y_hi, z), col: 16 (over x, y_lo, core).
Axes of the slice: x: 4, y: 4 (y_hi: 2, y_lo: 2; y = y_hi * 2 + y_lo), z: 4, core: 2. Of those that a mesh axis runs over, the one named last changes fastest.
Arguments:
- activations: bfloat16 [8192, 8192], P('col', 'row'), may hold values from -6 to 6
- out_grads: bfloat16 [8192, 4096], P('row', 'col'), may hold values from -0.0625 to 0.0625
- statistics: float32 [8, 16, 512, 1024], P('row', 'col'), may hold values from -10 to 200, as said below
Outputs:
- new_statistics: float32 [8, 16, 512, 1024], P('row', 'col')
- update: bfloat16 [8192, 4096], P('row', 'col')
Inputs may be any that keep to these rules, and one draw needn't show every extreme that they name: `statistics`: every statistic is symmetric and positive definite.
All inputs are finite; a program needn't handle non-finite values.
Results may differ from a plain program's by a relative error of at most 0.0017.
The roundings to bfloat16 on the way count: a program that leaves them out, or rounds other values in their place, can miss the bound.
Values may be sent and summed in bfloat16 or wider, within the bound.
No kernel may reach another device: no remote copies, remote signals or barrier semaphores. Data moves between devices by JAX's collectives and lax.ppermute only.
A program may use at most 128 MiB of HBM per device.

v0:
```python
import jax
import jax.numpy as jnp
from jax import lax
from jax.experimental import pallas as pl
from jax.experimental.pallas import tpu as pltpu
from jax.sharding import Mesh
from jax.sharding import PartitionSpec as P


DAMP = 10.0 ** (-3)
DECAY = 0.9
EPS = 1e-06
F32 = jnp.float32
BF16 = jnp.bfloat16
TILE = 256
SIZES = (512, 512)


VMEM = pl.BlockSpec(memory_space=pltpu.VMEM)
SMEM = pl.BlockSpec(memory_space=pltpu.SMEM)


def shift(value, axis, step):
    count = lax.axis_size(axis)
    return lax.ppermute(value, axis, [(k, (k + step) % count) for k in range(count)])


def aligned(start, size):
    return pl.ds(pl.multiple_of(start, size), size)


def split(value):
    high = value.astype(BF16)
    return high, (value - high.astype(F32)).astype(BF16)


def put_left(left, rows, cols, value):
    n = left.shape[0]
    high, low = split(value)
    left[rows, cols] = high
    left[rows, n + cols.start : n + cols.stop] = high
    left[rows, 2 * n + cols.start : 2 * n + cols.stop] = low


def put_right(right, rows, cols, value):
    n = right.shape[1]
    high, low = split(value)
    right[rows, cols] = high
    right[n + rows.start : n + rows.stop, cols] = low
    right[2 * n + rows.start : 2 * n + rows.stop, cols] = high


def put_symmetric(put, target, j, upper):
    start = j * TILE
    cols = slice(start, start + TILE)
    put(target, slice(0, start + TILE), cols, upper)
    for i in range(j):
        part = slice(i * TILE, (i + 1) * TILE)
        put(target, cols, part, upper[part, :].T)


def symmetric_product(left, right, emit):
    for j in range(right.shape[1] // TILE):
        start = j * TILE
        upper = jnp.dot(
            left[: start + TILE, :], right[:, start : start + TILE], preferred_element_type=F32
        )
        emit(j, upper)


def square_kernel(where, own, other, factor, square, stat, left, right):
    n = stat.shape[0]
    half = n // 2
    h = where[0]
    mine, his = aligned(h * half, half), aligned((1 - h) * half, half)
    stat[mine, :] = own[...]
    step, start, width = other.shape[0], 0, half
    for k in range(half // other.shape[0]):
        rows = aligned((1 - h) * half + k * step, step)
        stat[rows, aligned((1 - h) * half + k * step, step)] = other[:, start : start + step]
        for j in range(1, width // step):
            cols = aligned((1 - h) * half + (k + j) * step, step)
            block = other[:, start + j * step : start + (j + 1) * step]
            stat[rows, cols] = block
            stat[cols, rows] = block.T
        start, width = start + width, width - step
    stat[his, mine] = own[:, his].T

    row = lax.broadcasted_iota(jnp.int32, (TILE, TILE), 0)
    eye = row == lax.broadcasted_iota(jnp.int32, (TILE, TILE), 1)

    def sums(k, carry):
        trace, most = carry
        cols = aligned(k * TILE, TILE)
        trace += jnp.sum(jnp.where(eye, stat[cols, cols], 0.0))
        return trace, jnp.maximum(most, jnp.max(jnp.sum(jnp.abs(stat[:, cols]), axis=0)))

    trace, most = lax.fori_loop(0, n // TILE, sums, (F32(0.0), F32(0.0)))
    damping = DAMP * trace / n
    inverse = 1.0 / (most + damping)
    for i in range(n // TILE):
        rows = slice(i * TILE, (i + 1) * TILE)
        for j in range(n // TILE):
            cols = slice(j * TILE, (j + 1) * TILE)
            value = -stat[rows, cols] * inverse
            if i == j:
                value = jnp.where(eye, (1.25 - damping * inverse) + value, value)
            factor[rows, cols] = value
            put_left(left, rows, cols, value)
            put_right(right, rows, cols, value)

    def squared(j, upper):
        end = (j + 1) * TILE
        square[:end, j * TILE : end] = upper

    symmetric_product(left, right, squared)


def root_kernel(factor, square, root, left, right, left2, right2):
    for j in range(factor.shape[0] // TILE):
        end = (j + 1) * TILE
        upper = square[:end, j * TILE : end]
        put_symmetric(put_left, left2, j, upper)
        put_symmetric(put_right, right2, j, upper)

    def fourth(j, upper):
        end = (j + 1) * TILE
        cols = slice(j * TILE, end)
        put_symmetric(put_left, left, j, upper)
        put_symmetric(put_right, right, j, 5.0 * factor[:end, cols] - 4.0 * square[:end, cols])

    symmetric_product(left2, right2, fourth)

    def last(j, upper):
        end = (j + 1) * TILE
        cols = slice(j * TILE, end)
        value = 1.25 * factor[:end, cols] - 0.25 * upper
        root[:end, cols] = value.astype(BF16)
        for i in range(j):
            part = slice(i * TILE, (i + 1) * TILE)
            root[cols, part] = value[part, :].T.astype(BF16)

    symmetric_product(left, right, last)


def times(left, right):
    return jnp.dot(left, right, preferred_element_type=F32)


LAST = 6


def add_own(total, j, own, grads, part):
    half = grads.shape[1] // 2
    if j == 2:
        total[:, part] += times(grads[:, :half], own[3][...]) + times(grads[:, half:], own[4][...])
    else:
        total[:, part] += times(grads, own[(0, 1, 3, 2)[j]][...])


def own_kernel(slot, *refs):
    own, grads, (total, right, stack) = refs[:5], refs[5:12], refs[12:]
    tokens, width = right.shape[2], right.shape[1] // 2
    for k, piece in zip([k for k in range(8) if k != LAST], grads):
        stack[slot[k], :width, :] = piece[:tokens, :].T
        stack[slot[k], width:, :] = piece[tokens:, :].T
    right[...] = stack[4:]
    total[...] = jnp.zeros(total.shape, F32)
    for j in range(4):
        @pl.when(slot[LAST] != j)
        def _(j=j):
            add_own(total, j, own, stack[j], slice(None))


def partner_kernel(m):
    start = sum(SIZES[:m])

    def add(slot, own, pieces, right, before, late, total):
        value = before[:, start : start + total.shape[1]]
        for k in range(4):
            value += times(right[k], pieces[k][...])
        total[...] = value
        part = pl.ds(start, total.shape[1])
        views = [piece.at[:, part] for piece in own]
        for j in range(4):
            @pl.when(slot[LAST] == j)
            def _(j=j):
                add_own(total, j, views, late[...], slice(None))

    def first(slot, *refs):
        own, pieces, (last, right, before, total, full, late) = refs[:5], refs[5:9], refs[9:]
        tokens, width = right.shape[2], right.shape[1] // 2
        late[:width, :] = last[:tokens, :].T
        late[width:, :] = last[tokens:, :].T
        full[...] = right[...]

        @pl.when(slot[LAST] >= 4)
        def _():
            full[jnp.maximum(slot[LAST] - 4, 0)] = late[...]

        add(slot, own, pieces, full, before, late, total)

    def second(slot, *refs):
        own, pieces, (right, before, late, total) = refs[:5], refs[5:9], refs[9:]
        add(slot, own, pieces, right, before, late, total)

    return second if m else first


def gram_kernel(where, own, *refs):
    tiles, (renewed, block) = refs[:8], refs[8:]
    n = block.shape[0]
    width = tiles[0].shape[0]
    half = n // 2
    h, s = where[0], where[1]
    for dh in range(2):
        for ds in range(2):
            cols = aligned((2 * (h + dh - 2 * h * dh) + (s + ds - 2 * s * ds)) * width, width)
            block[cols, : SIZES[0]] = tiles[2 * dh + ds][...]
            block[cols, SIZES[0] :] = tiles[4 + 2 * dh + ds][...]
    rows = aligned(h * half, half)

    def renew(gram):
        renewed[...] = DECAY * own[...] + ((1.0 - DECAY) / n) * gram

    @pl.when(s == 0)
    def _():
        renew(lax.dot_general(
            block[:, rows], block[...], (((0,), (0,)), ((), ())), preferred_element_type=F32))

    @pl.when(s == 1)
    def _():
        renew(lax.dot_general(
            block[rows, :], block[...], (((1,), (1,)), ((), ())), preferred_element_type=F32))


def update_kernel(where, block, mine, other, update, cond):
    n, width = update.shape
    h, s = where[0], where[1]
    tile = aligned((2 * h + s) * width, width)

    def condition(left, right):
        product = times(right[tile, :], block[...]).astype(BF16)
        cond[...] = times(product, left[...])

    @pl.when(s == 0)
    def _():
        condition(mine, other)

    @pl.when(s == 1)
    def _():
        condition(other, mine)

    values = block[tile, :].astype(F32)
    conditioned = cond[...]
    count = n * width
    power = jnp.sum(values * values) / count
    base = jnp.sum(conditioned * conditioned) / count + EPS
    update[...] = (conditioned * jnp.sqrt(power / base)).astype(BF16).T


def resident(value):
    return pltpu.with_memory_space_constraint(value, pltpu.VMEM)


def call(kernel, out, args, in_specs, out_specs, scratch, flops, limit):
    return pl.pallas_call(
        kernel,
        out_shape=out,
        in_specs=in_specs,
        out_specs=out_specs,
        scratch_shapes=scratch,
        cost_estimate=pl.CostEstimate(flops=flops, transcendentals=0, bytes_accessed=2**23),
        compiler_params=pltpu.CompilerParams(vmem_limit_bytes=limit * 2**20),
    )(*[arg if spec is SMEM else resident(arg) for arg, spec in zip(args, in_specs)])


def root_of(where, own, other):
    n = own.shape[1]
    wide = pltpu.VMEM((n, n), F32)
    pair = [pltpu.VMEM((n, 3 * n), BF16), pltpu.VMEM((3 * n, n), BF16)]
    factor, square = call(
        square_kernel, (wide, wide), (where, own, other),
        [SMEM, VMEM, VMEM], (VMEM, VMEM), [wide] + pair, 4 * n**3, 20,
    )
    return call(
        root_kernel, pltpu.VMEM((n, n), BF16), (factor, square),
        [VMEM, VMEM], VMEM, pair + pair, 8 * n**3, 28,
    )


def own_gradient(slot, own, grads):
    tokens, rows = own[0].shape
    width = 2 * grads[0].shape[1]
    return call(
        own_kernel,
        (pltpu.VMEM((width, rows), F32), pltpu.VMEM((4, width, tokens), BF16)),
        (slot, *own, *grads), [SMEM] + [VMEM] * 12, (VMEM, VMEM),
        [pltpu.VMEM((8, width, tokens), BF16)], 8 * tokens * rows * width, 14,
    )


def whole_gradient(m, slot, own, partner, right, before, last):
    width, tokens = right.shape[1:]
    out = [pltpu.VMEM((width, SIZES[m]), F32)]
    args = (slot, *own, *partner, right, before, last)
    if m == 0:
        out += [pltpu.VMEM(right.shape, BF16), pltpu.VMEM((width, tokens), BF16)]
        args = (slot, *own, *partner, last, right, before)
    return call(
        partner_kernel(m), tuple(out), args, [SMEM] + [VMEM] * 12,
        (VMEM,) * len(out), [], 8 * tokens * SIZES[m] * width, 10,
    )


def finish(where, own, mine, other, tiles):
    n = mine.shape[0]
    half, width = n // 2, tiles[0].shape[0]
    renewed, block = call(
        gram_kernel, (jax.ShapeDtypeStruct((half, n), F32), pltpu.VMEM((n, n), BF16)),
        (where, own, *tiles), [SMEM] + [VMEM] * (1 + len(tiles)), (VMEM, VMEM), [], 2 * n**3, 12,
    )
    update = call(
        update_kernel, jax.ShapeDtypeStruct((n, width), BF16),
        (where, block, mine, other), [SMEM] + [VMEM] * 3, VMEM, [pltpu.VMEM((width, n), F32)],
        2 * n**3, 12,
    )
    return renewed, update


def step(activations, out_grads, statistics):
    own = statistics[0, 0]
    half, _ = own.shape
    width = out_grads.shape[1]
    x, z, yh = lax.axis_index("x"), lax.axis_index("z"), lax.axis_index("yh")
    h, s = lax.axis_index("yl"), lax.axis_index("core")
    where = jnp.stack([h, s]).astype(jnp.int32)

    cut = activations.shape[0] // 2
    below, above = shift(activations, "x", 1), shift(activations, "x", -1)
    far = [shift(below[:cut], "x", 1), shift(above[cut:], "x", -1)]
    mine = [activations, above, below] + far
    partner = []
    for m, size in enumerate(SIZES):
        start = sum(SIZES[:m])
        source = lax.optimization_barrier((activations, out_grads))[0] if m else activations
        across = shift(source[:, start : start + size], "yl", 1)
        below, above = shift(across, "x", 1), shift(across, "x", -1)
        last = shift(below, "x", 1) if m == 0 else shift(above, "x", -1)
        partner.append([across, above, last, below])

    tokens = out_grads.shape[0] // 2
    keep = lax.dynamic_slice_in_dim(out_grads, s * tokens, tokens, 0)
    give = lax.dynamic_slice_in_dim(out_grads, (1 - s) * tokens, tokens, 0)
    pair = jnp.concatenate([keep, shift(give, "core", 1)], 0)
    across = shift(pair, "yh", 1)
    below, above = shift(pair, "z", 1), shift(pair, "z", -1)
    grads = [pair, above, shift(below, "z", 1), below]
    below, above = shift(across, "z", 1), shift(across, "z", -1)
    grads += [across, above, shift(above, "z", -1), below]
    slot = []
    for dy in range(2):
        for dz in range(4):
            chunk = 4 * ((yh + dy) % 2) + (z + dz) % 4
            slot.append(4 * ((chunk + h) % 2) + (chunk // 2 - x) % 4)
    slot = jnp.stack(slot).astype(jnp.int32)

    quadrant = lax.dynamic_slice_in_dim(own, h * half, half, 1)
    cut = half // 4
    packed = [quadrant[k : k + cut, k:] for k in range(0, half, cut)]
    packed = jnp.concatenate(packed, 1)
    root = root_of(where, own, shift(packed, "yl", 1))
    other = shift(root, "core", 1)

    last = grads.pop(LAST)
    part, right = own_gradient(slot, mine, grads)
    tiles = []
    for m in range(2):
        if m == 0:
            total, right, last = whole_gradient(m, slot, mine, partner[m], right, part, last)
        else:
            (total,) = whole_gradient(m, slot, mine, partner[m], right, part, last)
        given = shift(total, "core", 1)
        tile = (total[:width] + given[width:]).astype(BF16)
        beside = (total[width:] + given[:width]).astype(BF16)
        across = shift(tile, "yl", 1)
        tiles += [tile, beside, across, shift(across, "core", 1)]

    renewed, update = finish(where, own, root, other, tiles)
    return renewed[None, None], update


def solution(mesh):
    torus = Mesh(mesh.devices.reshape(2, 4, 4, 2, 2), ("yh", "z", "x", "yl", "core"))
    row, col = ("yh", "z"), ("x", "yl", "core")
    return jax.shard_map(
        step,
        mesh=torus,
        in_specs=(P(col, row), P(row, col), P(row, col, None, None)),
        out_specs=(P(row, col, None, None), P(row, col)),
        check_vma=False,
    )
```

profile of v0, /device:TPU:0, one launch (start us, length us, event | category | flops | bytes accessed | tf_op | source)
XLA Modules:
  0.0 150.3 jit_solution(16273869562437213706)
XLA Ops:
  4.3 1.8 %collective-permute-start.26 = (f32[128,1280]{1,0:T(8,128)S(1)}, f32[128,1280]{1,0:T(8,128)S(1)}, u32[]{:S(2)}, u32[]{:S(2)}) collective-permute-start(f32[128,1280]{1,0:T(8,128)S(1)} %pad_maximum_fusion), channel_id=1, source_target_pairs={{0,2},{2,0},{1,3},{3,1},{4,6},{6,4},{5,7},{7,5},{8,10},{10,8},{9,1... | collective-permute-start | bytes 1966088 | tf_op jit(solution)/shard_map/ppermute | solution.py:25
  6.6 1.8 %collective-permute-start.19 = (bf16[512,512]{1,0:T(8,128)(2,1)S(1)}, bf16[512,512]{1,0:T(8,128)(2,1)}, u32[]{:S(2)}, u32[]{:S(2)}) collective-permute-start(bf16[512,512]{1,0:T(8,128)(2,1)S(1)} %slice.58), channel_id=1, source_target_pairs={{0,2},{2,0},{1,3},{3,1},{4,6},{6,4},{5,7},{7,5},{8,10},{10,8},{9,1... | collective-permute-start | bytes 1572872 | tf_op jit(solution)/shard_map/ppermute | solution.py:25
  8.3 2.8 %collective-permute-start = (bf16[512,1024]{1,0:T(8,128)(2,1)S(1)}, bf16[512,1024]{1,0:T(8,128)(2,1)S(1)}, u32[]{:S(2)}, u32[]{:S(2)}) collective-permute-start(bf16[512,1024]{1,0:T(8,128)(2,1)S(1)} %copy-done), channel_id=1, source_target_pairs={{0,12},{4,0},{8,4},{12,8},{1,13},{5,1},{9,5},{13,9},{2,14},{6,2},{... | collective-permute-start | bytes 3145736 | tf_op jit(solution)/shard_map/ppermute | solution.py:25
  12.1 21.2 %collective-permute-done.4.refs_5_ = bf16[512,512]{1,0:T(8,128)(2,1)} collective-permute-done((bf16[512,512]{1,0:T(8,128)(2,1)S(1)}, bf16[512,512]{1,0:T(8,128)(2,1)}, u32[]{:S(2)}, u32[]{:S(2)}) %collective-permute-start.4) | collective-permute-done | bytes 524320 | tf_op jit(solution)/shard_map/ppermute | solution.py:25
  33.3 3.3 %collective-permute-start.9 = (bf16[1024,256]{1,0:T(8,128)(2,1)S(1)}, bf16[1024,256]{1,0:T(8,128)(2,1)}, u32[]{:S(2)}, u32[]{:S(2)}) collective-permute-start(bf16[1024,256]{1,0:T(8,128)(2,1)S(1)} %pad_maximum_fusion.1.refs_5_), channel_id=1, source_target_pairs={{0,64},{64,0},{1,65},{65,1},{2,66},{66,2},{3,67},{67,3},{4,68},{68... | collective-permute-start | bytes 1572872 | tf_op jit(solution)/shard_map/ppermute | solution.py:25
  36.6 7.9 %collective-permute-done.19.refs_5_ = bf16[512,512]{1,0:T(8,128)(2,1)} collective-permute-done((bf16[512,512]{1,0:T(8,128)(2,1)S(1)}, bf16[512,512]{1,0:T(8,128)(2,1)}, u32[]{:S(2)}, u32[]{:S(2)}) %collective-permute-start.19) | collective-permute-done | bytes 524320 | tf_op jit(solution)/shard_map/ppermute | solution.py:25
  44.6 4.1 %collective-permute-start.12 = (bf16[1024,256]{1,0:T(8,128)(2,1)S(1)}, bf16[1024,256]{1,0:T(8,128)(2,1)S(1)}, u32[]{:S(2)}, u32[]{:S(2)}) collective-permute-start(bf16[1024,256]{1,0:T(8,128)(2,1)S(1)} %pad_maximum_fusion.1.refs_5_), channel_id=1, source_target_pairs={{0,48},{16,0},{32,16},{48,32},{1,49},{17,1},{33,17},{49,33},{2,50}... | collective-permute-start | bytes 1572872 | tf_op jit(solution)/shard_map/ppermute | solution.py:25
  50.4 7.5 %collective-permute-done.9.refs_9_ = bf16[1024,256]{1,0:T(8,128)(2,1)} collective-permute-done((bf16[1024,256]{1,0:T(8,128)(2,1)S(1)}, bf16[1024,256]{1,0:T(8,128)(2,1)}, u32[]{:S(2)}, u32[]{:S(2)}) %collective-permute-start.9) | collective-permute-done | bytes 524320 | tf_op jit(solution)/shard_map/ppermute | solution.py:25
  60.2 2.6 %collective-permute-start.20 = (bf16[512,512]{1,0:T(8,128)(2,1)}, bf16[512,512]{1,0:T(8,128)(2,1)}, u32[]{:S(2)}, u32[]{:S(2)}) collective-permute-start(bf16[512,512]{1,0:T(8,128)(2,1)} %collective-permute-done.19.refs_5_), channel_id=1, source_target_pairs={{0,12},{4,0},{8,4},{12,8},{1,13},{5,1},{9,5},{13,9},{2,14},{6,2},{... | collective-permute-start | bytes 1572872 | tf_op jit(solution)/shard_map/ppermute | solution.py:25
  63.5 2.9 %collective-permute-start.10 = (bf16[1024,256]{1,0:T(8,128)(2,1)}, bf16[1024,256]{1,0:T(8,128)(2,1)}, u32[]{:S(2)}, u32[]{:S(2)}) collective-permute-start(bf16[1024,256]{1,0:T(8,128)(2,1)} %collective-permute-done.9.refs_9_), channel_id=1, source_target_pairs={{0,48},{16,0},{32,16},{48,32},{1,49},{17,1},{33,17},{49,33},{2,50}... | collective-permute-start | bytes 1572872 | tf_op jit(solution)/shard_map/ppermute | solution.py:25
  68.4 4.4 %collective-permute-done.6.refs_8_ = bf16[512,512]{1,0:T(8,128)(2,1)} collective-permute-done((bf16[512,512]{1,0:T(8,128)(2,1)}, bf16[512,512]{1,0:T(8,128)(2,1)}, u32[]{:S(2)}, u32[]{:S(2)}) %collective-permute-start.6) | collective-permute-done | bytes 524320 | tf_op jit(solution)/shard_map/ppermute | solution.py:25
  73.6 3.0 %collective-permute-start.3 = (bf16[256,1024]{1,0:T(8,128)(2,1)}, bf16[256,1024]{1,0:T(8,128)(2,1)}, u32[]{:S(2)}, u32[]{:S(2)}) collective-permute-start(bf16[256,1024]{1,0:T(8,128)(2,1)} %slice.69), channel_id=1, source_target_pairs={{0,12},{4,0},{8,4},{12,8},{1,13},{5,1},{9,5},{13,9},{2,14},{6,2},{... | collective-permute-start | bytes 1572872 | tf_op jit(solution)/shard_map/ppermute | solution.py:25
  78.4 4.3 %collective-permute-done.14.refs_7_ = bf16[1024,256]{1,0:T(8,128)(2,1)} collective-permute-done((bf16[1024,256]{1,0:T(8,128)(2,1)}, bf16[1024,256]{1,0:T(8,128)(2,1)}, u32[]{:S(2)}, u32[]{:S(2)}) %collective-permute-start.14) | collective-permute-done | bytes 524320 | tf_op jit(solution)/shard_map/ppermute | solution.py:25
  82.8 8.6 %collective-permute-done.15.refs_11_ = bf16[1024,256]{1,0:T(8,128)(2,1)} collective-permute-done((bf16[1024,256]{1,0:T(8,128)(2,1)}, bf16[1024,256]{1,0:T(8,128)(2,1)}, u32[]{:S(2)}, u32[]{:S(2)}) %collective-permute-start.15) | collective-permute-done | bytes 524320 | tf_op jit(solution)/shard_map/ppermute | solution.py:25
  94.0 6.7 %shard_map.54 = (f32[1024,1024]{1,0:T(8,128)S(1)}, f32[1024,1024]{1,0:T(8,128)S(1)}) custom-call(s32[2]{0:T(128)S(1)} %pad_add_fusion.where, f32[512,1024]{1,0:T(8,128)S(1)} %bitcast.16, f32[128,1280]{1,0:T(8,128)S(1)} %copy-done.6), custom_call_target="tpu_custom_call" | custom-call | flops 4294967296 | bytes 8388608 | tf_op jit(solution)/shard_map/pallas_call | solution.py:267
  101.3 3.0 %collective-permute-start.21 = (bf16[512,512]{1,0:T(8,128)(2,1)}, bf16[512,512]{1,0:T(8,128)(2,1)S(1)}, u32[]{:S(2)}, u32[]{:S(2)}) collective-permute-start(bf16[512,512]{1,0:T(8,128)(2,1)} %collective-permute-done.20.refs_6_), channel_id=1, source_target_pairs={{0,12},{4,0},{8,4},{12,8},{1,13},{5,1},{9,5},{13,9},{2,14},{6,2},{... | collective-permute-start | bytes 1572872 | tf_op jit(solution)/shard_map/ppermute | solution.py:25
  104.3 5.4 %shard_map.50 = (f32[512,1024]{1,0:T(8,128)S(1)}, bf16[4,512,512]{2,1,0:T(8,128)(2,1)S(1)}) custom-call(s32[8]{0:T(128)S(1)} %stack.47.slot, bf16[512,1024]{1,0:T(8,128)(2,1)S(1)} %copy-done, bf16[512,1024]{1,0:T(8,128)(2,1)S(1)} %collective-permute-done.refs_1_, bf16[512,1024]{1,0:T(8,128)(2,1)S(1)} %collective-permute-done.1.refs_2_, ...), custom_call_target="tpu_custom_call" | custom-call | flops 2147483648 | bytes 8388608 | tf_op jit(solution)/shard_map/pallas_call | solution.py:267
  109.7 3.5 %shard_map.51 = (f32[512,512]{1,0:T(8,128)S(1)}, bf16[4,512,512]{2,1,0:T(8,128)(2,1)S(1)}, bf16[512,512]{1,0:T(8,128)(2,1)S(1)}) custom-call(s32[8]{0:T(128)S(1)} %stack.47.slot, bf16[512,1024]{1,0:T(8,128)(2,1)S(1)} %copy-done, bf16[512,1024]{1,0:T(8,128)(2,1)S(1)} %collective-permute-done.refs_1_, bf16[512,1024]{1,0:T(8,128)(2,1)S(1)} %collective-permute-done.1.refs_2_, ...), custom_call_target="tpu_custom_call" | custom-call | flops 1073741824 | bytes 8388608 | tf_op jit(solution)/shard_map/pallas_call | solution.py:267
  113.5 9.7 %shard_map.55.mine = bf16[1024,1024]{1,0:T(8,128)(2,1)S(1)} custom-call(f32[1024,1024]{1,0:T(8,128)S(1)} %get-tuple-element.20.factor, f32[1024,1024]{1,0:T(8,128)S(1)} %get-tuple-element.21.square), custom_call_target="tpu_custom_call" | custom-call | flops 8589934592 | bytes 8388608 | tf_op jit(solution)/shard_map/pallas_call | solution.py:267
  123.8 3.2 %shard_map.52 = f32[512,512]{1,0:T(8,128)S(1)} custom-call(s32[8]{0:T(128)S(1)} %stack.47.slot, bf16[512,1024]{1,0:T(8,128)(2,1)S(1)} %copy-done, bf16[512,1024]{1,0:T(8,128)(2,1)S(1)} %collective-permute-done.refs_1_, bf16[512,1024]{1,0:T(8,128)(2,1)S(1)} %collective-permute-done.1.refs_2_, bf16[256,1024]{1,0:T(8,128)(2,1)} %collective-permute-done.2.refs_3_, ...), custom_call_target="tpu_custom_call" | custom-call | flops 1073741824 | bytes 8388608 | tf_op jit(solution)/shard_map/pallas_call | solution.py:267
  131.0 5.7 %collective-permute-done.17.refs_2_ = bf16[256,512]{1,0:T(8,128)(2,1)S(1)} collective-permute-done((bf16[256,512]{1,0:T(8,128)(2,1)S(1)}, bf16[256,512]{1,0:T(8,128)(2,1)S(1)}, u32[]{:S(2)}, u32[]{:S(2)}) %collective-permute-start.17) | collective-permute-done | bytes 262176 | tf_op jit(solution)/shard_map/ppermute | solution.py:25
  136.7 5.1 %collective-permute-done.24.refs_6_ = bf16[256,512]{1,0:T(8,128)(2,1)S(1)} collective-permute-done((bf16[256,512]{1,0:T(8,128)(2,1)S(1)}, bf16[256,512]{1,0:T(8,128)(2,1)S(1)}, u32[]{:S(2)}, u32[]{:S(2)}) %collective-permute-start.24) | collective-permute-done | bytes 262176 | tf_op jit(solution)/shard_map/ppermute | solution.py:25
  143.4 3.6 %shard_map.53 = (f32[512,1024]{1,0:T(8,128)}, bf16[1024,1024]{1,0:T(8,128)(2,1)S(1)}) custom-call(s32[2]{0:T(128)S(1)} %pad_add_fusion.where, f32[512,1024]{1,0:T(8,128)S(1)} %bitcast.17, bf16[256,512]{1,0:T(8,128)(2,1)S(1)} %get-tuple-element.25.refs_0_, bf16[256,512]{1,0:T(8,128)(2,1)S(1)} %get-tuple-element.24.refs_1_, ...), custom_call_target="tpu_custom_call" | custom-call | flops 2147483648 | bytes 8388608 | tf_op jit(solution)/shard_map/pallas_call | solution.py:267
  147.0 3.3 %shard_map.56 = bf16[1024,256]{1,0:T(8,128)(2,1)} custom-call(s32[2]{0:T(128)S(1)} %pad_add_fusion.where, bf16[1024,1024]{1,0:T(8,128)(2,1)S(1)} %get-tuple-element.19.block, bf16[1024,1024]{1,0:T(8,128)(2,1)S(1)} %shard_map.55.mine, bf16[1024,1024]{1,0:T(8,128)(2,1)S(1)} %collective-permute-done.27.other), custom_call_target="tpu_custom_call" | custom-call | flops 2147483648 | bytes 8388608 | tf_op jit(solution)/shard_map/pallas_call | solution.py:267
  (73 shorter events, 23.8 us)
Async XLA Ops:
  1.7 9.4 %collective-permute-start.8 = (bf16[512,256]{1,0:T(8,128)(2,1)S(1)}, bf16[512,256]{1,0:T(8,128)(2,1)}, u32[]{:S(2)}, u32[]{:S(2)}) collective-permute-start(bf16[512,256]{1,0:T(8,128)(2,1)S(1)} %get-tuple-element.27), channel_id=1, source_target_pairs={{0,1},{1,0},{2,3},{3,2},{4,5},{5,4},{6,7},{7,6},{8,9},{9,8},{10,11... | collective-permute-start | bytes 786440 | tf_op jit(solution)/shard_map/ppermute | solution.py:25
  4.3 44.4 %collective-permute-start.26 = (f32[128,1280]{1,0:T(8,128)S(1)}, f32[128,1280]{1,0:T(8,128)S(1)}, u32[]{:S(2)}, u32[]{:S(2)}) collective-permute-start(f32[128,1280]{1,0:T(8,128)S(1)} %pad_maximum_fusion), channel_id=1, source_target_pairs={{0,2},{2,0},{1,3},{3,1},{4,6},{6,4},{5,7},{7,5},{8,10},{10,8},{9,1... | collective-permute-start | bytes 1966088 | tf_op jit(solution)/shard_map/ppermute | solution.py:25
  6.1 27.2 %collective-permute-start.4 = (bf16[512,512]{1,0:T(8,128)(2,1)S(1)}, bf16[512,512]{1,0:T(8,128)(2,1)}, u32[]{:S(2)}, u32[]{:S(2)}) collective-permute-start(bf16[512,512]{1,0:T(8,128)(2,1)S(1)} %slice.53), channel_id=1, source_target_pairs={{0,2},{2,0},{1,3},{3,1},{4,6},{6,4},{5,7},{7,5},{8,10},{10,8},{9,1... | collective-permute-start | bytes 1572872 | tf_op jit(solution)/shard_map/ppermute | solution.py:25
  6.6 38.0 %collective-permute-start.19 = (bf16[512,512]{1,0:T(8,128)(2,1)S(1)}, bf16[512,512]{1,0:T(8,128)(2,1)}, u32[]{:S(2)}, u32[]{:S(2)}) collective-permute-start(bf16[512,512]{1,0:T(8,128)(2,1)S(1)} %slice.58), channel_id=1, source_target_pairs={{0,2},{2,0},{1,3},{3,1},{4,6},{6,4},{5,7},{7,5},{8,10},{10,8},{9,1... | collective-permute-start | bytes 1572872 | tf_op jit(solution)/shard_map/ppermute | solution.py:25
  8.3 58.1 %collective-permute-start = (bf16[512,1024]{1,0:T(8,128)(2,1)S(1)}, bf16[512,1024]{1,0:T(8,128)(2,1)S(1)}, u32[]{:S(2)}, u32[]{:S(2)}) collective-permute-start(bf16[512,1024]{1,0:T(8,128)(2,1)S(1)} %copy-done), channel_id=1, source_target_pairs={{0,12},{4,0},{8,4},{12,8},{1,13},{5,1},{9,5},{13,9},{2,14},{6,2},{... | collective-permute-start | bytes 3145736 | tf_op jit(solution)/shard_map/ppermute | solution.py:25
  11.1 55.3 %collective-permute-start.1 = (bf16[512,1024]{1,0:T(8,128)(2,1)S(1)}, bf16[512,1024]{1,0:T(8,128)(2,1)S(1)}, u32[]{:S(2)}, u32[]{:S(2)}) collective-permute-start(bf16[512,1024]{1,0:T(8,128)(2,1)S(1)} %copy-done), channel_id=1, source_target_pairs={{0,4},{4,8},{8,12},{12,0},{1,5},{5,9},{9,13},{13,1},{2,6},{6,10},{... | collective-permute-start | bytes 3145736 | tf_op jit(solution)/shard_map/ppermute | solution.py:25
  33.3 24.5 %collective-permute-start.9 = (bf16[1024,256]{1,0:T(8,128)(2,1)S(1)}, bf16[1024,256]{1,0:T(8,128)(2,1)}, u32[]{:S(2)}, u32[]{:S(2)}) collective-permute-start(bf16[1024,256]{1,0:T(8,128)(2,1)S(1)} %pad_maximum_fusion.1.refs_5_), channel_id=1, source_target_pairs={{0,64},{64,0},{1,65},{65,1},{2,66},{66,2},{3,67},{67,3},{4,68},{68... | collective-permute-start | bytes 1572872 | tf_op jit(solution)/shard_map/ppermute | solution.py:25
  44.6 14.8 %collective-permute-start.12 = (bf16[1024,256]{1,0:T(8,128)(2,1)S(1)}, bf16[1024,256]{1,0:T(8,128)(2,1)S(1)}, u32[]{:S(2)}, u32[]{:S(2)}) collective-permute-start(bf16[1024,256]{1,0:T(8,128)(2,1)S(1)} %pad_maximum_fusion.1.refs_5_), channel_id=1, source_target_pairs={{0,48},{16,0},{32,16},{48,32},{1,49},{17,1},{33,17},{49,33},{2,50}... | collective-permute-start | bytes 1572872 | tf_op jit(solution)/shard_map/ppermute | solution.py:25
  49.6 14.0 %collective-permute-start.13 = (bf16[1024,256]{1,0:T(8,128)(2,1)S(1)}, bf16[1024,256]{1,0:T(8,128)(2,1)}, u32[]{:S(2)}, u32[]{:S(2)}) collective-permute-start(bf16[1024,256]{1,0:T(8,128)(2,1)S(1)} %pad_maximum_fusion.1.refs_5_), channel_id=1, source_target_pairs={{0,16},{16,32},{32,48},{48,0},{1,17},{17,33},{33,49},{49,1},{2,18}... | collective-permute-start | bytes 1572872 | tf_op jit(solution)/shard_map/ppermute | solution.py:25
  57.9 15.0 %collective-permute-start.6 = (bf16[512,512]{1,0:T(8,128)(2,1)}, bf16[512,512]{1,0:T(8,128)(2,1)}, u32[]{:S(2)}, u32[]{:S(2)}) collective-permute-start(bf16[512,512]{1,0:T(8,128)(2,1)} %collective-permute-done.4.refs_5_), channel_id=1, source_target_pairs={{0,4},{4,8},{8,12},{12,0},{1,5},{5,9},{9,13},{13,1},{2,6},{6,10},{... | collective-permute-start | bytes 1572872 | tf_op jit(solution)/shard_map/ppermute | solution.py:25
  60.2 13.5 %collective-permute-start.20 = (bf16[512,512]{1,0:T(8,128)(2,1)}, bf16[512,512]{1,0:T(8,128)(2,1)}, u32[]{:S(2)}, u32[]{:S(2)}) collective-permute-start(bf16[512,512]{1,0:T(8,128)(2,1)} %collective-permute-done.19.refs_5_), channel_id=1, source_target_pairs={{0,12},{4,0},{8,4},{12,8},{1,13},{5,1},{9,5},{13,9},{2,14},{6,2},{... | collective-permute-start | bytes 1572872 | tf_op jit(solution)/shard_map/ppermute | solution.py:25
  63.5 13.2 %collective-permute-start.10 = (bf16[1024,256]{1,0:T(8,128)(2,1)}, bf16[1024,256]{1,0:T(8,128)(2,1)}, u32[]{:S(2)}, u32[]{:S(2)}) collective-permute-start(bf16[1024,256]{1,0:T(8,128)(2,1)} %collective-permute-done.9.refs_9_), channel_id=1, source_target_pairs={{0,48},{16,0},{32,16},{48,32},{1,49},{17,1},{33,17},{49,33},{2,50}... | collective-permute-start | bytes 1572872 | tf_op jit(solution)/shard_map/ppermute | solution.py:25
  66.4 16.3 %collective-permute-start.14 = (bf16[1024,256]{1,0:T(8,128)(2,1)}, bf16[1024,256]{1,0:T(8,128)(2,1)}, u32[]{:S(2)}, u32[]{:S(2)}) collective-permute-start(bf16[1024,256]{1,0:T(8,128)(2,1)} %collective-permute-done.13.refs_8_), channel_id=1, source_target_pairs={{0,16},{16,32},{32,48},{48,0},{1,17},{17,33},{33,49},{49,1},{2,18}... | collective-permute-start | bytes 1572872 | tf_op jit(solution)/shard_map/ppermute | solution.py:25
  66.4 24.9 %collective-permute-start.15 = (bf16[1024,256]{1,0:T(8,128)(2,1)}, bf16[1024,256]{1,0:T(8,128)(2,1)}, u32[]{:S(2)}, u32[]{:S(2)}) collective-permute-start(bf16[1024,256]{1,0:T(8,128)(2,1)} %collective-permute-done.9.refs_9_), channel_id=1, source_target_pairs={{0,16},{16,32},{32,48},{48,0},{1,17},{17,33},{33,49},{49,1},{2,18}... | collective-permute-start | bytes 1572872 | tf_op jit(solution)/shard_map/ppermute | solution.py:25
  72.8 27.9 %collective-permute-start.2 = (bf16[256,1024]{1,0:T(8,128)(2,1)}, bf16[256,1024]{1,0:T(8,128)(2,1)}, u32[]{:S(2)}, u32[]{:S(2)}) collective-permute-start(bf16[256,1024]{1,0:T(8,128)(2,1)} %slice.68), channel_id=1, source_target_pairs={{0,4},{4,8},{8,12},{12,0},{1,5},{5,9},{9,13},{13,1},{2,6},{6,10},{... | collective-permute-start | bytes 1572872 | tf_op jit(solution)/shard_map/ppermute | solution.py:25
  73.6 27.7 %collective-permute-start.3 = (bf16[256,1024]{1,0:T(8,128)(2,1)}, bf16[256,1024]{1,0:T(8,128)(2,1)}, u32[]{:S(2)}, u32[]{:S(2)}) collective-permute-start(bf16[256,1024]{1,0:T(8,128)(2,1)} %slice.69), channel_id=1, source_target_pairs={{0,12},{4,0},{8,4},{12,8},{1,13},{5,1},{9,5},{13,9},{2,14},{6,2},{... | collective-permute-start | bytes 1572872 | tf_op jit(solution)/shard_map/ppermute | solution.py:25
  76.8 32.9 %collective-permute-start.5 = (bf16[512,512]{1,0:T(8,128)(2,1)}, bf16[512,512]{1,0:T(8,128)(2,1)S(1)}, u32[]{:S(2)}, u32[]{:S(2)}) collective-permute-start(bf16[512,512]{1,0:T(8,128)(2,1)} %collective-permute-done.4.refs_5_), channel_id=1, source_target_pairs={{0,12},{4,0},{8,4},{12,8},{1,13},{5,1},{9,5},{13,9},{2,14},{6,2},{... | collective-permute-start | bytes 1572872 | tf_op jit(solution)/shard_map/ppermute | solution.py:25
  82.8 26.9 %collective-permute-start.7 = (bf16[512,512]{1,0:T(8,128)(2,1)}, bf16[512,512]{1,0:T(8,128)(2,1)S(1)}, u32[]{:S(2)}, u32[]{:S(2)}) collective-permute-start(bf16[512,512]{1,0:T(8,128)(2,1)} %collective-permute-done.6.refs_8_), channel_id=1, source_target_pairs={{0,4},{4,8},{8,12},{12,0},{1,5},{5,9},{9,13},{13,1},{2,6},{6,10},{... | collective-permute-start | bytes 1572872 | tf_op jit(solution)/shard_map/ppermute | solution.py:25
  91.3 18.4 %collective-permute-start.11 = (bf16[1024,256]{1,0:T(8,128)(2,1)}, bf16[1024,256]{1,0:T(8,128)(2,1)S(1)}, u32[]{:S(2)}, u32[]{:S(2)}) collective-permute-start(bf16[1024,256]{1,0:T(8,128)(2,1)} %collective-permute-done.10.refs_10_), channel_id=1, source_target_pairs={{0,48},{16,0},{32,16},{48,32},{1,49},{17,1},{33,17},{49,33},{2,50}... | collective-permute-start | bytes 1572872 | tf_op jit(solution)/shard_map/ppermute | solution.py:25
  100.8 23.1 %collective-permute-start.22 = (bf16[512,512]{1,0:T(8,128)(2,1)}, bf16[512,512]{1,0:T(8,128)(2,1)S(1)}, u32[]{:S(2)}, u32[]{:S(2)}) collective-permute-start(bf16[512,512]{1,0:T(8,128)(2,1)} %collective-permute-done.19.refs_5_), channel_id=1, source_target_pairs={{0,4},{4,8},{8,12},{12,0},{1,5},{5,9},{9,13},{13,1},{2,6},{6,10},{... | collective-permute-start | bytes 1572872 | tf_op jit(solution)/shard_map/ppermute | solution.py:25
  101.3 22.5 %collective-permute-start.21 = (bf16[512,512]{1,0:T(8,128)(2,1)}, bf16[512,512]{1,0:T(8,128)(2,1)S(1)}, u32[]{:S(2)}, u32[]{:S(2)}) collective-permute-start(bf16[512,512]{1,0:T(8,128)(2,1)} %collective-permute-done.20.refs_6_), channel_id=1, source_target_pairs={{0,12},{4,0},{8,4},{12,8},{1,13},{5,1},{9,5},{13,9},{2,14},{6,2},{... | collective-permute-start | bytes 1572872 | tf_op jit(solution)/shard_map/ppermute | solution.py:25
  113.2 14.0 %collective-permute-start.16 = (f32[512,512]{1,0:T(8,128)S(1)}, f32[512,512]{1,0:T(8,128)S(1)}, u32[]{:S(2)}, u32[]{:S(2)}) collective-permute-start(f32[512,512]{1,0:T(8,128)S(1)} %get-tuple-element.14), channel_id=1, source_target_pairs={{0,1},{1,0},{2,3},{3,2},{4,5},{5,4},{6,7},{7,6},{8,9},{9,8},{10,11... | collective-permute-start | bytes 3145736 | tf_op jit(solution)/shard_map/ppermute | solution.py:25
  123.2 23.8 %collective-permute-start.27 = (bf16[1024,1024]{1,0:T(8,128)(2,1)S(1)}, bf16[1024,1024]{1,0:T(8,128)(2,1)S(1)}, u32[]{:S(2)}, u32[]{:S(2)}) collective-permute-start(bf16[1024,1024]{1,0:T(8,128)(2,1)S(1)} %shard_map.55.mine), channel_id=1, source_target_pairs={{0,1},{1,0},{2,3},{3,2},{4,5},{5,4},{6,7},{7,6},{8,9},{9,8},{10,11... | collective-permute-start | bytes 6291464 | tf_op jit(solution)/shard_map/ppermute | solution.py:25
  130.1 11.8 %collective-permute-start.24 = (bf16[256,512]{1,0:T(8,128)(2,1)S(1)}, bf16[256,512]{1,0:T(8,128)(2,1)S(1)}, u32[]{:S(2)}, u32[]{:S(2)}) collective-permute-start(bf16[256,512]{1,0:T(8,128)(2,1)S(1)} %get-tuple-element.23.refs_4_), channel_id=1, source_target_pairs={{0,2},{2,0},{1,3},{3,1},{4,6},{6,4},{5,7},{7,5},{8,10},{10,8},{9,1... | collective-permute-start | bytes 786440 | tf_op jit(solution)/shard_map/ppermute | solution.py:25
  (13 other events, 64.9 us)
where the time goes:
time: 152 us; the launch traced here: 150 us
  waiting for transfers between devices  69 us (45%)
  Pallas kernels  35.5 us (23%)
  starting transfers between devices  32.6 us (21%)
  local copies, waits for them, and re-layouts  10.4 us (7%)
  other arithmetic  1.62 us (1%)
    ppermute x28, waiting for transfers between devices, shift(): lax.ppermute(value, axis, [(k, (k + step) % count) for k in range(count)])  69 us
    pallas_call x7, Pallas kernels, call(): pl.pallas_call(kernel, out_shape=out, in_specs=in_specs, out_specs=out_sp...  35.5 us
    ppermute x28, starting transfers between devices, shift(): lax.ppermute(value, axis, [(k, (k + step) % count) for k in range(count)])  32.6 us
    unnamed x18, local copies, waits for them, and re-layouts  5.15 us
  transfers between devices with their start and end apart: 28, of which 12 were waited for; matrix products, arithmetic and copies ran while one was open for 4% of the time, Pallas kernels for 21%

commit v1 on v0

--- a/solution.py
+++ b/solution.py
@@ -13,7 +13,7 @@
 F32 = jnp.float32
 BF16 = jnp.bfloat16
 TILE = 256
-SIZES = (512, 512)
+SIZES = (640, 384)
 
 
 VMEM = pl.BlockSpec(memory_space=pltpu.VMEM)
@@ -343,8 +343,7 @@
     partner = []
     for m, size in enumerate(SIZES):
         start = sum(SIZES[:m])
-        source = lax.optimization_barrier((activations, out_grads))[0] if m else activations
-        across = shift(source[:, start : start + size], "yl", 1)
+        across = shift(activations[:, start : start + size], "yl", 1)
         below, above = shift(across, "x", 1), shift(across, "x", -1)
         last = shift(below, "x", 1) if m == 0 else shift(above, "x", -1)
         partner.append([across, above, last, below])

time: 152 us -> 151 us (level)
  waiting for transfers between devices: 69 us -> 62.4 us
  starting transfers between devices: 32.6 us -> 37.3 us
    ppermute x28, waiting for transfers between devices: 69 us -> 62.4 us  [shift(): lax.ppermute(value, axis, [(k, (k + step) % count) for k in range(count)])]
    ppermute x28, starting transfers between devices: 32.6 us -> 37.3 us  [shift(): lax.ppermute(value, axis, [(k, (k + step) % count) for k in range(count)])]
    slice x2, local copies, waits for them, and re-layouts: 0.07 us -> 2.02 us  [step(): across = shift(activations[:, start:start + size], 'yl', 1)]
    unnamed x18 -> x32, local copies, waits for them, and re-layouts: 5.15 us -> 4.89 us
  transfers between devices with their start and end apart: 28 -> 28, of which waited for: 12 -> 10; matrix products, arithmetic and copies ran while one was open for 4% -> 4% of each run, Pallas kernels for 21% -> 22%
where the time goes in v1:
time: 151 us; the launch traced here: 150 us
  waiting for transfers between devices  62.4 us (41%)
  starting transfers between devices  37.3 us (25%)
  Pallas kernels  36.3 us (24%)
  local copies, waits for them, and re-layouts  11.1 us (7%)
    ppermute x28, waiting for transfers between devices, shift(): lax.ppermute(value, axis, [(k, (k + step) % count) for k in range(count)])  62.4 us
    ppermute x28, starting transfers between devices, shift(): lax.ppermute(value, axis, [(k, (k + step) % count) for k in range(count)])  37.3 us
    pallas_call x7, Pallas kernels, call(): pl.pallas_call(kernel, out_shape=out, in_specs=in_specs, out_specs=out_sp...  36.3 us
    unnamed x32, local copies, waits for them, and re-layouts  4.89 us
  transfers between devices with their start and end apart: 28, of which 10 were waited for; matrix products, arithmetic and copies ran while one was open for 4% of the time, Pallas kernels for 22%

profile of v1, /device:TPU:0, one launch (start us, length us, event | category | flops | bytes accessed | tf_op | source)
XLA Modules:
  0.0 149.5 jit_solution(1930872278142044865)
XLA Ops:
  0.6 2.0 %slice.53 = bf16[512,640]{1,0:T(8,128)(2,1)} slice(bf16[512,1024]{1,0:T(8,128)(2,1)} %refs_0_.5), slice={[0:512], [0:640]} | slice | bytes 1310720 | tf_op jit(solution)/shard_map/slice | solution.py:346
  8.2 1.8 %collective-permute-start.19 = (bf16[512,384]{1,0:T(8,128)(2,1)S(1)}, bf16[512,384]{1,0:T(8,128)(2,1)S(1)}, u32[]{:S(2)}, u32[]{:S(2)}) collective-permute-start(bf16[512,384]{1,0:T(8,128)(2,1)S(1)} %slice.58), channel_id=1, source_target_pairs={{0,2},{2,0},{1,3},{3,1},{4,6},{6,4},{5,7},{7,5},{8,10},{10,8},{9,1... | collective-permute-start | bytes 1179656 | tf_op jit(solution)/shard_map/ppermute | solution.py:25
  10.0 2.8 %collective-permute-start = (bf16[512,1024]{1,0:T(8,128)(2,1)S(1)}, bf16[512,1024]{1,0:T(8,128)(2,1)S(1)}, u32[]{:S(2)}, u32[]{:S(2)}) collective-permute-start(bf16[512,1024]{1,0:T(8,128)(2,1)S(1)} %copy-done), channel_id=1, source_target_pairs={{0,12},{4,0},{8,4},{12,8},{1,13},{5,1},{9,5},{13,9},{2,14},{6,2},{... | collective-permute-start | bytes 3145736 | tf_op jit(solution)/shard_map/ppermute | solution.py:25
  12.8 28.9 %collective-permute-done.19.refs_5_ = bf16[512,384]{1,0:T(8,128)(2,1)S(1)} collective-permute-done((bf16[512,384]{1,0:T(8,128)(2,1)S(1)}, bf16[512,384]{1,0:T(8,128)(2,1)S(1)}, u32[]{:S(2)}, u32[]{:S(2)}) %collective-permute-start.19) | collective-permute-done | bytes 393248 | tf_op jit(solution)/shard_map/ppermute | solution.py:25
  41.7 3.4 %collective-permute-start.9 = (bf16[1024,256]{1,0:T(8,128)(2,1)S(1)}, bf16[1024,256]{1,0:T(8,128)(2,1)}, u32[]{:S(2)}, u32[]{:S(2)}) collective-permute-start(bf16[1024,256]{1,0:T(8,128)(2,1)S(1)} %pad_maximum_fusion.1.refs_5_), channel_id=1, source_target_pairs={{0,64},{64,0},{1,65},{65,1},{2,66},{66,2},{3,67},{67,3},{4,68},{68... | collective-permute-start | bytes 1572872 | tf_op jit(solution)/shard_map/ppermute | solution.py:25
  45.1 4.0 %collective-permute-start.12 = (bf16[1024,256]{1,0:T(8,128)(2,1)S(1)}, bf16[1024,256]{1,0:T(8,128)(2,1)S(1)}, u32[]{:S(2)}, u32[]{:S(2)}) collective-permute-start(bf16[1024,256]{1,0:T(8,128)(2,1)S(1)} %pad_maximum_fusion.1.refs_5_), channel_id=1, source_target_pairs={{0,48},{16,0},{32,16},{48,32},{1,49},{17,1},{33,17},{49,33},{2,50}... | collective-permute-start | bytes 1572872 | tf_op jit(solution)/shard_map/ppermute | solution.py:25
  49.9 6.3 %collective-permute-done.9.refs_9_ = bf16[1024,256]{1,0:T(8,128)(2,1)} collective-permute-done((bf16[1024,256]{1,0:T(8,128)(2,1)S(1)}, bf16[1024,256]{1,0:T(8,128)(2,1)}, u32[]{:S(2)}, u32[]{:S(2)}) %collective-permute-start.9) | collective-permute-done | bytes 524320 | tf_op jit(solution)/shard_map/ppermute | solution.py:25
  60.0 3.7 %collective-permute-start.10 = (bf16[1024,256]{1,0:T(8,128)(2,1)}, bf16[1024,256]{1,0:T(8,128)(2,1)S(1)}, u32[]{:S(2)}, u32[]{:S(2)}) collective-permute-start(bf16[1024,256]{1,0:T(8,128)(2,1)} %collective-permute-done.9.refs_9_), channel_id=1, source_target_pairs={{0,48},{16,0},{32,16},{48,32},{1,49},{17,1},{33,17},{49,33},{2,50}... | collective-permute-start | bytes 1572872 | tf_op jit(solution)/shard_map/ppermute | solution.py:25
  63.7 2.8 %collective-permute-start.20 = (bf16[512,384]{1,0:T(8,128)(2,1)S(1)}, bf16[512,384]{1,0:T(8,128)(2,1)S(1)}, u32[]{:S(2)}, u32[]{:S(2)}) collective-permute-start(bf16[512,384]{1,0:T(8,128)(2,1)S(1)} %collective-permute-done.19.refs_5_), channel_id=1, source_target_pairs={{0,12},{4,0},{8,4},{12,8},{1,13},{5,1},{9,5},{13,9},{2,14},{6,2},{... | collective-permute-start | bytes 1179656 | tf_op jit(solution)/shard_map/ppermute | solution.py:25
  68.2 4.4 %collective-permute-done.20.refs_6_ = bf16[512,384]{1,0:T(8,128)(2,1)S(1)} collective-permute-done((bf16[512,384]{1,0:T(8,128)(2,1)S(1)}, bf16[512,384]{1,0:T(8,128)(2,1)S(1)}, u32[]{:S(2)}, u32[]{:S(2)}) %collective-permute-start.20) | collective-permute-done | bytes 393248 | tf_op jit(solution)/shard_map/ppermute | solution.py:25
  73.4 3.7 %collective-permute-start.5 = (bf16[512,640]{1,0:T(8,128)(2,1)}, bf16[512,640]{1,0:T(8,128)(2,1)}, u32[]{:S(2)}, u32[]{:S(2)}) collective-permute-start(bf16[512,640]{1,0:T(8,128)(2,1)} %collective-permute-done.4.refs_5_), channel_id=1, source_target_pairs={{0,12},{4,0},{8,4},{12,8},{1,13},{5,1},{9,5},{13,9},{2,14},{6,2},{... | collective-permute-start | bytes 1966088 | tf_op jit(solution)/shard_map/ppermute | solution.py:25
  77.1 3.2 %collective-permute-start.3 = (bf16[256,1024]{1,0:T(8,128)(2,1)}, bf16[256,1024]{1,0:T(8,128)(2,1)}, u32[]{:S(2)}, u32[]{:S(2)}) collective-permute-start(bf16[256,1024]{1,0:T(8,128)(2,1)} %slice.69), channel_id=1, source_target_pairs={{0,12},{4,0},{8,4},{12,8},{1,13},{5,1},{9,5},{13,9},{2,14},{6,2},{... | collective-permute-start | bytes 1572872 | tf_op jit(solution)/shard_map/ppermute | solution.py:25
  82.4 5.2 %collective-permute-done.15.refs_11_ = bf16[1024,256]{1,0:T(8,128)(2,1)} collective-permute-done((bf16[1024,256]{1,0:T(8,128)(2,1)}, bf16[1024,256]{1,0:T(8,128)(2,1)}, u32[]{:S(2)}, u32[]{:S(2)}) %collective-permute-start.15) | collective-permute-done | bytes 524320 | tf_op jit(solution)/shard_map/ppermute | solution.py:25
  89.2 7.3 %shard_map.54 = (f32[1024,1024]{1,0:T(8,128)S(1)}, f32[1024,1024]{1,0:T(8,128)S(1)}) custom-call(s32[2]{0:T(128)S(1)} %pad_add_fusion.where, f32[512,1024]{1,0:T(8,128)S(1)} %bitcast.16, f32[128,1280]{1,0:T(8,128)} %collective-permute-done.26.other), custom_call_target="tpu_custom_call" | custom-call | flops 4294967296 | bytes 8388608 | tf_op jit(solution)/shard_map/pallas_call | solution.py:267
  96.6 1.7 %collective-permute-start.22 = (bf16[512,384]{1,0:T(8,128)(2,1)S(1)}, bf16[512,384]{1,0:T(8,128)(2,1)S(1)}, u32[]{:S(2)}, u32[]{:S(2)}) collective-permute-start(bf16[512,384]{1,0:T(8,128)(2,1)S(1)} %collective-permute-done.19.refs_5_), channel_id=1, source_target_pairs={{0,4},{4,8},{8,12},{12,0},{1,5},{5,9},{9,13},{13,1},{2,6},{6,10},{... | collective-permute-start | bytes 1179656 | tf_op jit(solution)/shard_map/ppermute | solution.py:25
  99.7 3.7 %collective-permute-start.21 = (bf16[512,384]{1,0:T(8,128)(2,1)S(1)}, bf16[512,384]{1,0:T(8,128)(2,1)S(1)}, u32[]{:S(2)}, u32[]{:S(2)}) collective-permute-start(bf16[512,384]{1,0:T(8,128)(2,1)S(1)} %copy-done.6), channel_id=1, source_target_pairs={{0,12},{4,0},{8,4},{12,8},{1,13},{5,1},{9,5},{13,9},{2,14},{6,2},{... | collective-permute-start | bytes 1179656 | tf_op jit(solution)/shard_map/ppermute | solution.py:25
  103.4 4.9 %shard_map.50 = (f32[512,1024]{1,0:T(8,128)S(1)}, bf16[4,512,512]{2,1,0:T(8,128)(2,1)S(1)}) custom-call(s32[8]{0:T(128)S(1)} %stack.47.slot, bf16[512,1024]{1,0:T(8,128)(2,1)S(1)} %copy-done, bf16[512,1024]{1,0:T(8,128)(2,1)S(1)} %collective-permute-done.refs_1_, bf16[512,1024]{1,0:T(8,128)(2,1)S(1)} %collective-permute-done.1.refs_2_, ...), custom_call_target="tpu_custom_call" | custom-call | flops 2147483648 | bytes 8388608 | tf_op jit(solution)/shard_map/pallas_call | solution.py:267
  108.4 4.7 %shard_map.51 = (f32[512,640]{1,0:T(8,128)S(1)}, bf16[4,512,512]{2,1,0:T(8,128)(2,1)S(1)}, bf16[512,512]{1,0:T(8,128)(2,1)S(1)}) custom-call(s32[8]{0:T(128)S(1)} %stack.47.slot, bf16[512,1024]{1,0:T(8,128)(2,1)S(1)} %copy-done, bf16[512,1024]{1,0:T(8,128)(2,1)S(1)} %collective-permute-done.refs_1_, bf16[512,1024]{1,0:T(8,128)(2,1)S(1)} %collective-permute-done.1.refs_2_, ...), custom_call_target="tpu_custom_call" | custom-call | flops 1342177280 | bytes 8388608 | tf_op jit(solution)/shard_map/pallas_call | solution.py:267
  113.4 9.6 %shard_map.55.mine = bf16[1024,1024]{1,0:T(8,128)(2,1)S(1)} custom-call(f32[1024,1024]{1,0:T(8,128)S(1)} %get-tuple-element.18.factor, f32[1024,1024]{1,0:T(8,128)S(1)} %get-tuple-element.19.square), custom_call_target="tpu_custom_call" | custom-call | flops 8589934592 | bytes 8388608 | tf_op jit(solution)/shard_map/pallas_call | solution.py:267
  123.6 2.9 %shard_map.52 = f32[512,384]{1,0:T(8,128)S(1)} custom-call(s32[8]{0:T(128)S(1)} %stack.47.slot, bf16[512,1024]{1,0:T(8,128)(2,1)S(1)} %copy-done, bf16[512,1024]{1,0:T(8,128)(2,1)S(1)} %collective-permute-done.refs_1_, bf16[512,1024]{1,0:T(8,128)(2,1)S(1)} %collective-permute-done.1.refs_2_, bf16[256,1024]{1,0:T(8,128)(2,1)} %collective-permute-done.2.refs_3_, ...), custom_call_target="tpu_custom_call" | custom-call | flops 805306368 | bytes 8388608 | tf_op jit(solution)/shard_map/pallas_call | solution.py:267
  129.5 7.9 %collective-permute-done.17.refs_2_ = bf16[256,640]{1,0:T(8,128)(2,1)S(1)} collective-permute-done((bf16[256,640]{1,0:T(8,128)(2,1)S(1)}, bf16[256,640]{1,0:T(8,128)(2,1)S(1)}, u32[]{:S(2)}, u32[]{:S(2)}) %collective-permute-start.17) | collective-permute-done | bytes 327712 | tf_op jit(solution)/shard_map/ppermute | solution.py:25
  137.4 3.7 %collective-permute-done.24.refs_6_ = bf16[256,384]{1,0:T(8,128)(2,1)S(1)} collective-permute-done((bf16[256,384]{1,0:T(8,128)(2,1)S(1)}, bf16[256,384]{1,0:T(8,128)(2,1)S(1)}, u32[]{:S(2)}, u32[]{:S(2)}) %collective-permute-start.24) | collective-permute-done | bytes 196640 | tf_op jit(solution)/shard_map/ppermute | solution.py:25
  142.6 3.6 %shard_map.53 = (f32[512,1024]{1,0:T(8,128)}, bf16[1024,1024]{1,0:T(8,128)(2,1)S(1)}) custom-call(s32[2]{0:T(128)S(1)} %pad_add_fusion.where, f32[512,1024]{1,0:T(8,128)S(1)} %bitcast.17, bf16[256,640]{1,0:T(8,128)(2,1)S(1)} %get-tuple-element.21.refs_0_, bf16[256,640]{1,0:T(8,128)(2,1)S(1)} %get-tuple-element.20.refs_1_, ...), custom_call_target="tpu_custom_call" | custom-call | flops 2147483648 | bytes 8388608 | tf_op jit(solution)/shard_map/pallas_call | solution.py:267
  146.2 3.3 %shard_map.56 = bf16[1024,256]{1,0:T(8,128)(2,1)} custom-call(s32[2]{0:T(128)S(1)} %pad_add_fusion.where, bf16[1024,1024]{1,0:T(8,128)(2,1)S(1)} %get-tuple-element.17.block, bf16[1024,1024]{1,0:T(8,128)(2,1)S(1)} %shard_map.55.mine, bf16[1024,1024]{1,0:T(8,128)(2,1)S(1)} %collective-permute-done.27.other), custom_call_target="tpu_custom_call" | custom-call | flops 2147483648 | bytes 8388608 | tf_op jit(solution)/shard_map/pallas_call | solution.py:267
  (87 shorter events, 22.8 us)
Async XLA Ops:
  2.6 42.5 %collective-permute-start.4 = (bf16[512,640]{1,0:T(8,128)(2,1)}, bf16[512,640]{1,0:T(8,128)(2,1)}, u32[]{:S(2)}, u32[]{:S(2)}) collective-permute-start(bf16[512,640]{1,0:T(8,128)(2,1)} %slice.53), channel_id=1, source_target_pairs={{0,2},{2,0},{1,3},{3,1},{4,6},{6,4},{5,7},{7,5},{8,10},{10,8},{9,1... | collective-permute-start | bytes 1966088 | tf_op jit(solution)/shard_map/ppermute | solution.py:25
  7.7 41.4 %collective-permute-start.26 = (f32[128,1280]{1,0:T(8,128)}, f32[128,1280]{1,0:T(8,128)}, u32[]{:S(2)}, u32[]{:S(2)}) collective-permute-start(f32[128,1280]{1,0:T(8,128)} %pad_maximum_fusion), channel_id=1, source_target_pairs={{0,2},{2,0},{1,3},{3,1},{4,6},{6,4},{5,7},{7,5},{8,10},{10,8},{9,1... | collective-permute-start | bytes 1966088 | tf_op jit(solution)/shard_map/ppermute | solution.py:25
  8.2 33.5 %collective-permute-start.19 = (bf16[512,384]{1,0:T(8,128)(2,1)S(1)}, bf16[512,384]{1,0:T(8,128)(2,1)S(1)}, u32[]{:S(2)}, u32[]{:S(2)}) collective-permute-start(bf16[512,384]{1,0:T(8,128)(2,1)S(1)} %slice.58), channel_id=1, source_target_pairs={{0,2},{2,0},{1,3},{3,1},{4,6},{6,4},{5,7},{7,5},{8,10},{10,8},{9,1... | collective-permute-start | bytes 1179656 | tf_op jit(solution)/shard_map/ppermute | solution.py:25
  10.0 53.7 %collective-permute-start = (bf16[512,1024]{1,0:T(8,128)(2,1)S(1)}, bf16[512,1024]{1,0:T(8,128)(2,1)S(1)}, u32[]{:S(2)}, u32[]{:S(2)}) collective-permute-start(bf16[512,1024]{1,0:T(8,128)(2,1)S(1)} %copy-done), channel_id=1, source_target_pairs={{0,12},{4,0},{8,4},{12,8},{1,13},{5,1},{9,5},{13,9},{2,14},{6,2},{... | collective-permute-start | bytes 3145736 | tf_op jit(solution)/shard_map/ppermute | solution.py:25
  12.7 53.8 %collective-permute-start.1 = (bf16[512,1024]{1,0:T(8,128)(2,1)S(1)}, bf16[512,1024]{1,0:T(8,128)(2,1)S(1)}, u32[]{:S(2)}, u32[]{:S(2)}) collective-permute-start(bf16[512,1024]{1,0:T(8,128)(2,1)S(1)} %copy-done), channel_id=1, source_target_pairs={{0,4},{4,8},{8,12},{12,0},{1,5},{5,9},{9,13},{13,1},{2,6},{6,10},{... | collective-permute-start | bytes 3145736 | tf_op jit(solution)/shard_map/ppermute | solution.py:25
  41.7 14.5 %collective-permute-start.9 = (bf16[1024,256]{1,0:T(8,128)(2,1)S(1)}, bf16[1024,256]{1,0:T(8,128)(2,1)}, u32[]{:S(2)}, u32[]{:S(2)}) collective-permute-start(bf16[1024,256]{1,0:T(8,128)(2,1)S(1)} %pad_maximum_fusion.1.refs_5_), channel_id=1, source_target_pairs={{0,64},{64,0},{1,65},{65,1},{2,66},{66,2},{3,67},{67,3},{4,68},{68... | collective-permute-start | bytes 1572872 | tf_op jit(solution)/shard_map/ppermute | solution.py:25
  45.1 14.1 %collective-permute-start.12 = (bf16[1024,256]{1,0:T(8,128)(2,1)S(1)}, bf16[1024,256]{1,0:T(8,128)(2,1)S(1)}, u32[]{:S(2)}, u32[]{:S(2)}) collective-permute-start(bf16[1024,256]{1,0:T(8,128)(2,1)S(1)} %pad_maximum_fusion.1.refs_5_), channel_id=1, source_target_pairs={{0,48},{16,0},{32,16},{48,32},{1,49},{17,1},{33,17},{49,33},{2,50}... | collective-permute-start | bytes 1572872 | tf_op jit(solution)/shard_map/ppermute | solution.py:25
  49.1 14.5 %collective-permute-start.13 = (bf16[1024,256]{1,0:T(8,128)(2,1)S(1)}, bf16[1024,256]{1,0:T(8,128)(2,1)S(1)}, u32[]{:S(2)}, u32[]{:S(2)}) collective-permute-start(bf16[1024,256]{1,0:T(8,128)(2,1)S(1)} %pad_maximum_fusion.1.refs_5_), channel_id=1, source_target_pairs={{0,16},{16,32},{32,48},{48,0},{1,17},{17,33},{33,49},{49,1},{2,18}... | collective-permute-start | bytes 1572872 | tf_op jit(solution)/shard_map/ppermute | solution.py:25
  56.2 20.8 %collective-permute-start.6 = (bf16[512,640]{1,0:T(8,128)(2,1)}, bf16[512,640]{1,0:T(8,128)(2,1)}, u32[]{:S(2)}, u32[]{:S(2)}) collective-permute-start(bf16[512,640]{1,0:T(8,128)(2,1)} %collective-permute-done.4.refs_5_), channel_id=1, source_target_pairs={{0,4},{4,8},{8,12},{12,0},{1,5},{5,9},{9,13},{13,1},{2,6},{6,10},{... | collective-permute-start | bytes 1966088 | tf_op jit(solution)/shard_map/ppermute | solution.py:25
  60.0 17.1 %collective-permute-start.10 = (bf16[1024,256]{1,0:T(8,128)(2,1)}, bf16[1024,256]{1,0:T(8,128)(2,1)S(1)}, u32[]{:S(2)}, u32[]{:S(2)}) collective-permute-start(bf16[1024,256]{1,0:T(8,128)(2,1)} %collective-permute-done.9.refs_9_), channel_id=1, source_target_pairs={{0,48},{16,0},{32,16},{48,32},{1,49},{17,1},{33,17},{49,33},{2,50}... | collective-permute-start | bytes 1572872 | tf_op jit(solution)/shard_map/ppermute | solution.py:25
  63.7 16.7 %collective-permute-start.14 = (bf16[1024,256]{1,0:T(8,128)(2,1)S(1)}, bf16[1024,256]{1,0:T(8,128)(2,1)S(1)}, u32[]{:S(2)}, u32[]{:S(2)}) collective-permute-start(bf16[1024,256]{1,0:T(8,128)(2,1)S(1)} %collective-permute-done.13.refs_8_), channel_id=1, source_target_pairs={{0,16},{16,32},{32,48},{48,0},{1,17},{17,33},{33,49},{49,1},{2,18}... | collective-permute-start | bytes 1572872 | tf_op jit(solution)/shard_map/ppermute | solution.py:25
  63.7 8.9 %collective-permute-start.20 = (bf16[512,384]{1,0:T(8,128)(2,1)S(1)}, bf16[512,384]{1,0:T(8,128)(2,1)S(1)}, u32[]{:S(2)}, u32[]{:S(2)}) collective-permute-start(bf16[512,384]{1,0:T(8,128)(2,1)S(1)} %collective-permute-done.19.refs_5_), channel_id=1, source_target_pairs={{0,12},{4,0},{8,4},{12,8},{1,13},{5,1},{9,5},{13,9},{2,14},{6,2},{... | collective-permute-start | bytes 1179656 | tf_op jit(solution)/shard_map/ppermute | solution.py:25
  66.5 21.1 %collective-permute-start.15 = (bf16[1024,256]{1,0:T(8,128)(2,1)}, bf16[1024,256]{1,0:T(8,128)(2,1)}, u32[]{:S(2)}, u32[]{:S(2)}) collective-permute-start(bf16[1024,256]{1,0:T(8,128)(2,1)} %collective-permute-done.9.refs_9_), channel_id=1, source_target_pairs={{0,16},{16,32},{32,48},{48,0},{1,17},{17,33},{33,49},{49,1},{2,18}... | collective-permute-start | bytes 1572872 | tf_op jit(solution)/shard_map/ppermute | solution.py:25
  73.4 35.0 %collective-permute-start.5 = (bf16[512,640]{1,0:T(8,128)(2,1)}, bf16[512,640]{1,0:T(8,128)(2,1)}, u32[]{:S(2)}, u32[]{:S(2)}) collective-permute-start(bf16[512,640]{1,0:T(8,128)(2,1)} %collective-permute-done.4.refs_5_), channel_id=1, source_target_pairs={{0,12},{4,0},{8,4},{12,8},{1,13},{5,1},{9,5},{13,9},{2,14},{6,2},{... | collective-permute-start | bytes 1966088 | tf_op jit(solution)/shard_map/ppermute | solution.py:25
  77.1 19.5 %collective-permute-start.2 = (bf16[256,1024]{1,0:T(8,128)(2,1)}, bf16[256,1024]{1,0:T(8,128)(2,1)}, u32[]{:S(2)}, u32[]{:S(2)}) collective-permute-start(bf16[256,1024]{1,0:T(8,128)(2,1)} %slice.68), channel_id=1, source_target_pairs={{0,4},{4,8},{8,12},{12,0},{1,5},{5,9},{9,13},{13,1},{2,6},{6,10},{... | collective-permute-start | bytes 1572872 | tf_op jit(solution)/shard_map/ppermute | solution.py:25
  77.1 22.6 %collective-permute-start.3 = (bf16[256,1024]{1,0:T(8,128)(2,1)}, bf16[256,1024]{1,0:T(8,128)(2,1)}, u32[]{:S(2)}, u32[]{:S(2)}) collective-permute-start(bf16[256,1024]{1,0:T(8,128)(2,1)} %slice.69), channel_id=1, source_target_pairs={{0,12},{4,0},{8,4},{12,8},{1,13},{5,1},{9,5},{13,9},{2,14},{6,2},{... | collective-permute-start | bytes 1572872 | tf_op jit(solution)/shard_map/ppermute | solution.py:25
  81.2 27.2 %collective-permute-start.7 = (bf16[512,640]{1,0:T(8,128)(2,1)}, bf16[512,640]{1,0:T(8,128)(2,1)}, u32[]{:S(2)}, u32[]{:S(2)}) collective-permute-start(bf16[512,640]{1,0:T(8,128)(2,1)} %collective-permute-done.6.refs_8_), channel_id=1, source_target_pairs={{0,4},{4,8},{8,12},{12,0},{1,5},{5,9},{9,13},{13,1},{2,6},{6,10},{... | collective-permute-start | bytes 1966088 | tf_op jit(solution)/shard_map/ppermute | solution.py:25
  87.6 20.8 %collective-permute-start.11 = (bf16[1024,256]{1,0:T(8,128)(2,1)}, bf16[1024,256]{1,0:T(8,128)(2,1)S(1)}, u32[]{:S(2)}, u32[]{:S(2)}) collective-permute-start(bf16[1024,256]{1,0:T(8,128)(2,1)} %copy-done.11), channel_id=1, source_target_pairs={{0,48},{16,0},{32,16},{48,32},{1,49},{17,1},{33,17},{49,33},{2,50}... | collective-permute-start | bytes 1572872 | tf_op jit(solution)/shard_map/ppermute | solution.py:25
  96.6 27.0 %collective-permute-start.22 = (bf16[512,384]{1,0:T(8,128)(2,1)S(1)}, bf16[512,384]{1,0:T(8,128)(2,1)S(1)}, u32[]{:S(2)}, u32[]{:S(2)}) collective-permute-start(bf16[512,384]{1,0:T(8,128)(2,1)S(1)} %collective-permute-done.19.refs_5_), channel_id=1, source_target_pairs={{0,4},{4,8},{8,12},{12,0},{1,5},{5,9},{9,13},{13,1},{2,6},{6,10},{... | collective-permute-start | bytes 1179656 | tf_op jit(solution)/shard_map/ppermute | solution.py:25
  99.7 23.8 %collective-permute-start.21 = (bf16[512,384]{1,0:T(8,128)(2,1)S(1)}, bf16[512,384]{1,0:T(8,128)(2,1)S(1)}, u32[]{:S(2)}, u32[]{:S(2)}) collective-permute-start(bf16[512,384]{1,0:T(8,128)(2,1)S(1)} %copy-done.6), channel_id=1, source_target_pairs={{0,12},{4,0},{8,4},{12,8},{1,13},{5,1},{9,5},{13,9},{2,14},{6,2},{... | collective-permute-start | bytes 1179656 | tf_op jit(solution)/shard_map/ppermute | solution.py:25
  113.1 13.5 %collective-permute-start.16 = (f32[512,640]{1,0:T(8,128)S(1)}, f32[512,640]{1,0:T(8,128)S(1)}, u32[]{:S(2)}, u32[]{:S(2)}) collective-permute-start(f32[512,640]{1,0:T(8,128)S(1)} %get-tuple-element.13), channel_id=1, source_target_pairs={{0,1},{1,0},{2,3},{3,2},{4,5},{5,4},{6,7},{7,6},{8,9},{9,8},{10,11... | collective-permute-start | bytes 3932168 | tf_op jit(solution)/shard_map/ppermute | solution.py:25
  123.0 23.2 %collective-permute-start.27 = (bf16[1024,1024]{1,0:T(8,128)(2,1)S(1)}, bf16[1024,1024]{1,0:T(8,128)(2,1)S(1)}, u32[]{:S(2)}, u32[]{:S(2)}) collective-permute-start(bf16[1024,1024]{1,0:T(8,128)(2,1)S(1)} %shard_map.55.mine), channel_id=1, source_target_pairs={{0,1},{1,0},{2,3},{3,2},{4,5},{5,4},{6,7},{7,6},{8,9},{9,8},{10,11... | collective-permute-start | bytes 6291464 | tf_op jit(solution)/shard_map/ppermute | solution.py:25
  126.7 10.7 %collective-permute-start.17 = (bf16[256,640]{1,0:T(8,128)(2,1)S(1)}, bf16[256,640]{1,0:T(8,128)(2,1)S(1)}, u32[]{:S(2)}, u32[]{:S(2)}) collective-permute-start(bf16[256,640]{1,0:T(8,128)(2,1)S(1)} %get-tuple-element.21.refs_0_), channel_id=1, source_target_pairs={{0,2},{2,0},{1,3},{3,1},{4,6},{6,4},{5,7},{7,5},{8,10},{10,8},{9,1... | collective-permute-start | bytes 983048 | tf_op jit(solution)/shard_map/ppermute | solution.py:25
  129.0 12.2 %collective-permute-start.24 = (bf16[256,384]{1,0:T(8,128)(2,1)S(1)}, bf16[256,384]{1,0:T(8,128)(2,1)S(1)}, u32[]{:S(2)}, u32[]{:S(2)}) collective-permute-start(bf16[256,384]{1,0:T(8,128)(2,1)S(1)} %get-tuple-element.23.refs_4_), channel_id=1, source_target_pairs={{0,2},{2,0},{1,3},{3,1},{4,6},{6,4},{5,7},{7,5},{8,10},{10,8},{9,1... | collective-permute-start | bytes 589832 | tf_op jit(solution)/shard_map/ppermute | solution.py:25
  (20 other events, 139.1 us)
